TPU v7x, 32 devices: a whole 2x2x4 slice. The times are simulated.
32 devices in a mesh: owner: 4 (over y, x), rows: 8 (over z, core).
Axes of the slice: x: 2, y: 2, z: 4, core: 2. Of those that a mesh axis runs over, the one named last changes fastest.
Arguments:
- train_gate: float32 [64, 2048, 1024], P('owner', 'rows'), may hold values from -0.1875 to 0.1875
- train_up: float32 [64, 2048, 1024], P('owner', 'rows'), may hold values from -0.1875 to 0.1875
- train_down: float32 [64, 1024, 2048], P('owner', None, 'rows'), may hold values from -0.25 to 0.25
- router_weight: float32 [2048, 64], P('rows', 'owner'), may hold values from -0.125 to 0.125
- router_gain: float32 [2048], P('rows'), may hold values from 0.25 to 1.75
Outputs:
- ready_gate: bfloat16 [64, 2048, 1024], P('owner', None, 'rows')
- ready_up: bfloat16 [64, 2048, 1024], P('owner', None, 'rows')
- ready_down: bfloat16 [64, 1024, 2048], P('owner', 'rows')
- scale_gate: float32 [64, 1024], P('owner', 'rows')
- scale_up: float32 [64, 1024], P('owner', 'rows')
- scale_down: float32 [64, 1024], P('owner', 'rows')
- serve_router: bfloat16 [2048, 64], replicated
All inputs are finite; a program needn't handle non-finite values. Where the computation divides by a largest or mean magnitude, that divisor is 1e-20 or more.
Results may differ from a plain program's by a relative error of at most 0.0013.
Values may be sent and summed in bfloat16 or wider, within the bound.
A program may use at most 192 MiB of HBM per device.

v0:
```python
import jax
import jax.numpy as jnp
from jax import lax
from jax.sharding import PartitionSpec as P

D_MODEL = 2048


def local(train_gate, train_up, train_down, router_weight, router_gain):
    total_gate, total_up, total_down = lax.psum(
        (
            jnp.sum(jnp.abs(train_gate), axis=1),
            jnp.sum(jnp.abs(train_up), axis=1),
            jnp.sum(jnp.abs(train_down), axis=2),
        ),
        "rows",
    )
    scale_gate = total_gate / D_MODEL
    scale_up = total_up / D_MODEL
    scale_down = total_down / D_MODEL
    narrow_gate, narrow_up, narrow_down = (
        (train_gate / jnp.expand_dims(scale_gate, 1)).astype(jnp.bfloat16),
        (train_up / jnp.expand_dims(scale_up, 1)).astype(jnp.bfloat16),
        (train_down / jnp.expand_dims(scale_down, 2)).astype(jnp.bfloat16),
    )
    ready_gate, ready_up = (
        lax.all_to_all(narrow_gate, "rows", split_axis=2, concat_axis=1, tiled=True),
        lax.all_to_all(narrow_up, "rows", split_axis=2, concat_axis=1, tiled=True),
    )
    ready_down = lax.all_to_all(narrow_down, "rows", split_axis=1, concat_axis=2, tiled=True)
    scale_gate = lax.dynamic_slice_in_dim(
        scale_gate, lax.axis_index("rows") * ready_gate.shape[2], ready_gate.shape[2], axis=1
    )
    scale_up = lax.dynamic_slice_in_dim(
        scale_up, lax.axis_index("rows") * ready_up.shape[2], ready_up.shape[2], axis=1
    )
    scale_down = lax.dynamic_slice_in_dim(
        scale_down, lax.axis_index("rows") * ready_down.shape[1], ready_down.shape[1], axis=1
    )
    part_router = (router_weight * router_gain[:, None]).astype(jnp.bfloat16)
    row_router = lax.all_gather(part_router, "rows", axis=0, tiled=True)
    serve_router = lax.all_gather(row_router, "owner", axis=1, tiled=True)
    return (ready_gate, ready_up, ready_down, scale_gate, scale_up, scale_down, serve_router)


def solution(mesh):
    return jax.shard_map(
        local,
        mesh=mesh,
        in_specs=(
            P("owner", "rows", None),
            P("owner", "rows", None),
            P("owner", None, "rows"),
            P("rows", "owner"),
            P("rows"),
        ),
        out_specs=(
            P("owner", None, "rows"),
            P("owner", None, "rows"),
            P("owner", "rows", None),
            P("owner", "rows"),
            P("owner", "rows"),
            P("owner", "rows"),
            P(),
        ),
        check_vma=False,
    )
```

profile of v0, /device:TPU:0, one launch (start us, length us, event | category | flops | bytes accessed | tf_op | source)
XLA Modules:
  0.0 737.8 jit_solution(7608499507201470121)
XLA Ops:
  7.2 0.0 all-reduce.3.cloned.1.call-start
  7.2 8.6 %abs_reduce_fusion = f32[16,1024]{1,0:T(8,128)} fusion(f32[16,1024,256]{2,1,0:T(8,128)} %param.7), kind=kLoop, calls=%fused_computation.2 | loop fusion | flops 8372224 | bytes 16842752 | tf_op jit(solution)/shard_map/reduce_sum | solution.py:14
  15.8 12.6 %abs_reduce_fusion.1 = (f32[16,1024]{1,0:T(8,128)}, f32[16,1024]{1,0:T(8,128)}) fusion(f32[16,256,1024]{2,1,0:T(8,128)} %param.6, f32[16,256,1024]{2,1,0:T(8,128)} %param.5), kind=kLoop, calls=%fused_computation.4 | loop fusion | flops 16744448 | bytes 33685504 | tf_op jit(solution)/shard_map/reduce_sum | solution.py:13
  28.4 0.0 all-reduce.3.cloned.1.call-update
  28.4 17.6 %copy.19 = f32[16,256,1024]{1,0,2:T(8,128)} copy(f32[16,256,1024]{2,1,0:T(8,128)} %param.6) | data formatting | bytes 33554432 | tf_op args[1]
  46.1 40.7 %all-reduce.3.cloned.1.call-done = (f32[16,1024]{1,0:T(8,128)}, f32[16,1024]{1,0:T(8,128)}, f32[16,1024]{1,0:T(8,128)}) async-done(((f32[16,1024]{1,0:T(8,128)}, f32[16,1024]{1,0:T(8,128)}, f32[16,1024]{1,0:T(8,128)}), (f32[16,1024]{1,0:T(8,128)}, f32[16,1024]{1,0:T(8,128)}, f32[16,1024]{1,0:T(8,128)})) %all-reduce.3.cloned.1.call-update) | async-done | bytes 196624 | tf_op jit(solution)/shard_map/psum | solution.py:10
  86.8 0.8 broadcast_multiply_fusion.1
  87.6 0.2 copy.18
  87.8 9.6 %divide_convert_fusion = bf16[16,256,1024]{1,0,2:T(8,128)(2,1)} fusion(f32[16,256,1024]{1,0,2:T(8,128)} %copy.19, f32[16,1024]{0,1:T(8,128)S(1)} %copy.18), kind=kLoop, calls=%fused_computation.3 | loop fusion | flops 8388608 | bytes 25231360 | tf_op jit(solution)/shard_map/convert_element_type | solution.py:23
  97.5 4.9 all-to-all-start.1
  102.4 17.6 %copy.16 = f32[16,256,1024]{1,0,2:T(8,128)} copy(f32[16,256,1024]{2,1,0:T(8,128)} %param.5) | data formatting | bytes 33554432 | tf_op args[0]
  120.0 0.2 copy.15
  120.3 9.7 %divide_convert_fusion.1 = bf16[16,256,1024]{1,0,2:T(8,128)(2,1)} fusion(f32[16,256,1024]{1,0,2:T(8,128)} %copy.16, f32[16,1024]{0,1:T(8,128)S(1)} %copy.15), kind=kLoop, calls=%fused_computation.5 | loop fusion | flops 8388608 | bytes 25231360 | tf_op jit(solution)/shard_map/convert_element_type | solution.py:22
  129.9 156.3 %all-to-all-done.1 = bf16[16,256,1024]{1,0,2:T(8,128)(2,1)} async-done(((bf16[16,256,1024]{1,0,2:T(8,128)(2,1)}), bf16[16,256,1024]{1,0,2:T(8,128)(2,1)}, u32[]{:S(2)}, u32[]{:S(2)}) %all-to-all-start.1) | async-done | bytes 8388640 | tf_op jit(solution)/shard_map/all_to_all | solution.py:28
  286.3 4.9 all-to-all-start
  291.2 0.2 copy.21
  291.4 0.0 copy-start.2
  291.4 0.0 copy-start.3
  291.5 16.6 %fusion = bf16[16,1024,256]{2,0,1:T(8,128)(2,1)} fusion(f32[16,1024,256]{2,1,0:T(8,128)} %param.7, f32[16,1024]{0,1:T(8,128)S(1)} %copy.21), kind=kLoop, calls=%fused_computation.1 | loop fusion | flops 8388608 | bytes 25231360 | tf_op jit(solution)/shard_map/convert_element_type | solution.py:24
  308.1 167.0 %all-to-all-done = bf16[16,256,1024]{1,0,2:T(8,128)(2,1)} async-done(((bf16[16,256,1024]{1,0,2:T(8,128)(2,1)}), bf16[16,256,1024]{1,0,2:T(8,128)(2,1)}, u32[]{:S(2)}, u32[]{:S(2)}) %all-to-all-start) | async-done | bytes 8388640 | tf_op jit(solution)/shard_map/all_to_all | solution.py:27
  475.1 5.0 all-to-all-start.2
  480.1 189.9 %all_gather.6 = bf16[2048,16]{0,1:T(8,128)(2,1)S(1)} all-gather(bf16[256,16]{0,1:T(8,128)(2,1)S(1)} %multiply_convert_fusion), channel_id=1, replica_groups=mesh['owner'=4,'rows'=8] {'rows'}, dimensions={0}, use_global_device_ids=true | all-gather | bytes 73728 | tf_op jit(solution)/shard_map/all_gather | solution.py:41
  670.0 9.1 %all_gather.7 = bf16[2048,64]{0,1:T(8,128)(2,1)S(1)} all-gather(bf16[2048,16]{0,1:T(8,128)(2,1)S(1)} %all_gather.6), channel_id=1, replica_groups=mesh['owner'=4,'rows'=8] {'owner'}, dimensions={1}, use_global_device_ids=true | all-gather | bytes 327680 | tf_op jit(solution)/shard_map/all_gather | solution.py:42
  679.1 0.6 constant_dynamic-slice_fusion
  679.7 0.6 constant_dynamic-slice_fusion.1
  680.3 0.6 constant_dynamic-slice_fusion.2
  680.9 12.3 %copy.20 = bf16[16,8,256,128]{3,2,1,0:T(8,128)(2,1)} copy(bf16[16,8,256,128]{2,0,3,1:T(8,128)(2,1)} %bitcast.4) | data formatting | bytes 16777216 | tf_op jit(solution)/shard_map/all_to_all | solution.py:28
  693.2 12.3 %copy.17 = bf16[16,8,256,128]{3,2,1,0:T(8,128)(2,1)} copy(bf16[16,8,256,128]{2,0,3,1:T(8,128)(2,1)} %bitcast.1) | data formatting | bytes 16777216 | tf_op jit(solution)/shard_map/all_to_all | solution.py:27
  705.5 0.0 all-to-all-done.2
  705.5 11.4 %copy.23 = bf16[16,128,8,256]{3,2,1,0:T(8,128)(2,1)} copy(bf16[16,128,8,256]{3,0,1,2:T(8,128)(2,1)} %bitcast.7) | data formatting | bytes 16777216 | tf_op jit(solution)/shard_map/all_to_all | solution.py:30
  716.9 13.4 %all_to_all.50 = bf16[16,128,2048]{2,1,0:T(8,128)(2,1)} reshape(bf16[16,128,8,256]{3,2,1,0:T(8,128)(2,1)} %copy.23) | data formatting | bytes 16777216 | tf_op jit(solution)/shard_map/all_to_all | solution.py:30
  730.3 0.7 copy.31
  (9 shorter events, 0.0 us)
Async XLA Ops:
  7.2 79.6 %all-reduce.3.cloned.1.call-start = ((), (), s32[]{:S(2)}) async-start(), calls=%async_computation.3 | async-start | bytes 393216 | tf_op jit(solution)/shard_map/psum | solution.py:10
  97.5 188.8 %all-to-all-start.1 = ((bf16[16,256,1024]{1,0,2:T(8,128)(2,1)}), bf16[16,256,1024]{1,0,2:T(8,128)(2,1)}, u32[]{:S(2)}, u32[]{:S(2)}) async-start(bf16[16,256,1024]{1,0,2:T(8,128)(2,1)} %divide_convert_fusion), calls=%async_computation.1 | async-start | bytes 16777216 | tf_op jit(solution)/shard_map/all_to_all | solution.py:28
  102.4 17.6 %copy-start.1 = (f32[16,1024]{1,0:T(8,128)S(1)}, f32[16,1024]{1,0:T(8,128)}, u32[]{:S(2)}) copy-start(f32[16,1024]{1,0:T(8,128)} %get-tuple-element.7) | copy-start | bytes 196612
  120.2 171.0 %copy-start = (f32[16,1024]{1,0:T(8,128)S(1)}, f32[16,1024]{1,0:T(8,128)}, u32[]{:S(2)}) copy-start(f32[16,1024]{1,0:T(8,128)} %get-tuple-element.9) | copy-start | bytes 196612
  286.3 188.8 %all-to-all-start = ((bf16[16,256,1024]{1,0,2:T(8,128)(2,1)}), bf16[16,256,1024]{1,0,2:T(8,128)(2,1)}, u32[]{:S(2)}, u32[]{:S(2)}) async-start(bf16[16,256,1024]{1,0,2:T(8,128)(2,1)} %divide_convert_fusion.1), calls=%async_computation | async-start | bytes 16777216 | tf_op jit(solution)/shard_map/all_to_all | solution.py:27
  291.4 188.7 %copy-start.2 = (f32[256,16]{0,1:T(8,128)S(1)}, f32[256,16]{0,1:T(8,128)}, u32[]{:S(2)}) copy-start(f32[256,16]{0,1:T(8,128)} %param.8) | copy-start | bytes 49156
  291.4 188.7 %copy-start.3 = (f32[256]{0:T(256)S(1)}, f32[256]{0:T(256)}, u32[]{:S(2)}) copy-start(f32[256]{0:T(256)} %param.9) | copy-start | bytes 3076
  475.1 230.4 %all-to-all-start.2 = ((bf16[16,1024,256]{2,0,1:T(8,128)(2,1)}), bf16[16,1024,256]{2,0,1:T(8,128)(2,1)}, u32[]{:S(2)}, u32[]{:S(2)}) async-start(bf16[16,1024,256]{2,0,1:T(8,128)(2,1)} %fusion), calls=%async_computation.2 | async-start | bytes 16777216 | tf_op jit(solution)/shard_map/all_to_all | solution.py:30
Sparse Core Ops, SparseCore 0:
  28.6 58.1 all-reduce.2
where the time goes:
time: 740 us; the launch traced here: 738 us
  waiting for transfers between devices  364 us (49%)
  blocking collectives  199 us (27%)
  local copies, waits for them, and re-layouts  87.7 us (12%)
  other arithmetic  58 us (8%)
  starting transfers between devices  14.9 us (2%)
  between operations  14.2 us (2%)
    all_gather x1, blocking collectives, local(): row_router = lax.all_gather(part_router, 'rows', axis=0, tiled=True)  190 us
    all_to_all x1, waiting for transfers between devices, local(): lax.all_to_all(narrow_gate, 'rows', split_axis=2, concat_axis=1, tiled=True)  167 us
    all_to_all x1, waiting for transfers between devices, local(): lax.all_to_all(narrow_up, 'rows', split_axis=2, concat_axis=1, tiled=True)  156 us
    psum x1, waiting for transfers between devices, local(): lax.psum((jnp.sum(jnp.abs(train_gate), axis=1), jnp.sum(jnp.abs(train_up)...  40.7 us
    unnamed x11, local copies, waits for them, and re-layouts  36 us
    all_to_all x2, local copies, waits for them, and re-layouts, local(): lax.all_to_all(narrow_down, 'rows', split_axis=1, concat_axis=2, tiled=True)  24.8 us
    convert_element_type x1, other arithmetic, local(): (train_down / jnp.expand_dims(scale_down, 2)).astype(jnp.bfloat16)  16.6 us
  transfers between devices with their start and end apart: 4, of which 3 were waited for; matrix products, arithmetic and copies ran while one was open for 12% of the time, Pallas kernels for 0%

commit v1 on v0

--- a/solution.py
+++ b/solution.py
@@ -24,7 +24,12 @@
         (train_down / jnp.expand_dims(scale_down, 2)).astype(jnp.bfloat16),
     )
     ready_gate, ready_up = (
-        lax.all_to_all(narrow_gate, "rows", split_axis=2, concat_axis=1, tiled=True),
+        jnp.concatenate(
+            lax.all_to_all(
+                jnp.stack(jnp.split(narrow_gate, lax.axis_size("rows"), axis=2)), "rows", 0, 0
+            ),
+            axis=1,
+        ),
         lax.all_to_all(narrow_up, "rows", split_axis=2, concat_axis=1, tiled=True),
     )
     ready_down = lax.all_to_all(narrow_down, "rows", split_axis=1, concat_axis=2, tiled=True)

time: 740 us -> 742 us (level)
  waiting for transfers between devices: 364 us -> 382 us
  local copies, waits for them, and re-layouts: 87.7 us -> 75.5 us
    psum x1, waiting for transfers between devices: 40.7 us -> 58.3 us  [local(): lax.psum((jnp.sum(jnp.abs(train_gate), axis=1), jnp.sum(jnp.abs(train_up)...]
    all_to_all x1 -> x0, local copies, waits for them, and re-layouts: 12.3 us -> none  [local(): lax.all_to_all(narrow_gate, 'rows', split_axis=2, concat_axis=1, tiled=True)]
    all_to_all x1, waiting for transfers between devices: 156 us -> 167 us  [local(): lax.all_to_all(narrow_up, 'rows', split_axis=2, concat_axis=1, tiled=True)]
    all_to_all x1, waiting for transfers between devices: 167 us -> 156 us  [local(): lax.all_to_all(jnp.stack(jnp.split(narrow_gate, lax.axis_size('rows'), ax...]
    unnamed x11 -> x17, local copies, waits for them, and re-layouts: 36 us -> 27.1 us
    reshape x0 -> x1, local copies, waits for them, and re-layouts: none -> 7.89 us  [local(): jnp.concatenate(lax.all_to_all(jnp.stack(jnp.split(narrow_gate, lax.axis_...]
  transfers between devices with their start and end apart: 4 -> 4, of which waited for: 3 -> 3; matrix products, arithmetic and copies ran while one was open for 12% -> 9% of each run, Pallas kernels for 0% -> 0%
where the time goes in v1:
time: 742 us; the launch traced here: 741 us
  waiting for transfers between devices  382 us (51%)
  blocking collectives  199 us (27%)
  local copies, waits for them, and re-layouts  75.5 us (10%)
  other arithmetic  55.6 us (7%)
  starting transfers between devices  15.1 us (2%)
  between operations  14.1 us (2%)
    all_gather x1, blocking collectives, local(): row_router = lax.all_gather(part_router, 'rows', axis=0, tiled=True)  190 us
    all_to_all x1, waiting for transfers between devices, local(): lax.all_to_all(narrow_up, 'rows', split_axis=2, concat_axis=1, tiled=True)  167 us
    all_to_all x1, waiting for transfers between devices, local(): lax.all_to_all(jnp.stack(jnp.split(narrow_gate, lax.axis_size('rows'), ax...  156 us
    psum x1, waiting for transfers between devices, local(): lax.psum((jnp.sum(jnp.abs(train_gate), axis=1), jnp.sum(jnp.abs(train_up)...  58.3 us
    unnamed x17, local copies, waits for them, and re-layouts  27.1 us
    all_to_all x2, local copies, waits for them, and re-layouts, local(): lax.all_to_all(narrow_down, 'rows', split_axis=1, concat_axis=2, tiled=True)  24.8 us
    convert_element_type x1, other arithmetic, local(): (train_down / jnp.expand_dims(scale_down, 2)).astype(jnp.bfloat16)  16.6 us
  transfers between devices with their start and end apart: 4, of which 3 were waited for; matrix products, arithmetic and copies ran while one was open for 9% of the time, Pallas kernels for 0%

profile of v1, /device:TPU:0, one launch (start us, length us, event | category | flops | bytes accessed | tf_op | source)
XLA Modules:
  0.0 740.8 jit_solution(12766531883530185823)
XLA Ops:
  7.2 8.6 %abs_reduce_fusion = f32[16,1024]{1,0:T(8,128)} fusion(f32[16,1024,256]{2,1,0:T(8,128)} %param.7), kind=kLoop, calls=%fused_computation.2 | loop fusion | flops 8372224 | bytes 16842752 | tf_op jit(solution)/shard_map/reduce_sum | solution.py:14
  15.8 12.6 %abs_reduce_fusion.1 = (f32[16,1024]{1,0:T(8,128)}, f32[16,1024]{1,0:T(8,128)}) fusion(f32[16,256,1024]{2,1,0:T(8,128)} %param.6, f32[16,256,1024]{2,1,0:T(8,128)} %param.5), kind=kLoop, calls=%fused_computation.4 | loop fusion | flops 16744448 | bytes 33685504 | tf_op jit(solution)/shard_map/reduce_sum | solution.py:13
  28.4 58.3 %all-reduce.3.cloned.1.call-done = (f32[16,1024]{1,0:T(8,128)}, f32[16,1024]{1,0:T(8,128)}, f32[16,1024]{1,0:T(8,128)}) async-done(((f32[16,1024]{1,0:T(8,128)}, f32[16,1024]{1,0:T(8,128)}, f32[16,1024]{1,0:T(8,128)}), (f32[16,1024]{1,0:T(8,128)}, f32[16,1024]{1,0:T(8,128)}, f32[16,1024]{1,0:T(8,128)})) %all-reduce.3.cloned.1.call-update) | async-done | bytes 196624 | tf_op jit(solution)/shard_map/psum | solution.py:10
  86.8 0.8 broadcast_multiply_fusion.2
  87.6 7.2 divide_convert_fusion.1
  94.8 1.2 fusion.8
  96.1 1.2 fusion.7
  97.3 1.2 fusion.6
  98.6 1.2 fusion.5
  99.8 1.2 fusion.4
  101.1 1.2 fusion.3
  102.3 1.2 fusion.2
  103.6 1.2 fusion.1
  104.8 4.9 all-to-all-start
  109.8 17.6 %copy.17 = f32[16,256,1024]{1,0,2:T(8,128)} copy(f32[16,256,1024]{2,1,0:T(8,128)} %param.6) | data formatting | bytes 33554432 | tf_op args[1]
  127.4 0.2 copy.16
  127.6 9.6 %divide_convert_fusion = bf16[16,256,1024]{1,0,2:T(8,128)(2,1)} fusion(f32[16,256,1024]{1,0,2:T(8,128)} %copy.17, f32[16,1024]{0,1:T(8,128)S(1)} %copy.16), kind=kLoop, calls=%fused_computation.3 | loop fusion | flops 8388608 | bytes 25231360 | tf_op jit(solution)/shard_map/convert_element_type | solution.py:23
  137.3 156.4 %all-to-all-done = bf16[8,16,256,128]{3,2,1,0:T(8,128)(2,1)} async-done(((bf16[8,16,256,128]{3,2,1,0:T(8,128)(2,1)}), bf16[8,16,256,128]{3,2,1,0:T(8,128)(2,1)}, u32[]{:S(2)}, u32[]{:S(2)}) %all-to-all-start) | async-done | bytes 8388640 | tf_op jit(solution)/shard_map/all_to_all | solution.py:28
  293.6 4.9 all-to-all-start.1
  298.8 16.6 %fusion = bf16[16,1024,256]{2,0,1:T(8,128)(2,1)} fusion(f32[16,1024,256]{2,1,0:T(8,128)} %param.7, f32[16,1024]{0,1:T(8,128)S(1)} %copy.19), kind=kLoop, calls=%fused_computation.1 | loop fusion | flops 8388608 | bytes 25231360 | tf_op jit(solution)/shard_map/convert_element_type | solution.py:24
  315.5 167.0 %all-to-all-done.1 = bf16[16,256,1024]{1,0,2:T(8,128)(2,1)} async-done(((bf16[16,256,1024]{1,0,2:T(8,128)(2,1)}), bf16[16,256,1024]{1,0,2:T(8,128)(2,1)}, u32[]{:S(2)}, u32[]{:S(2)}) %all-to-all-start.1) | async-done | bytes 8388640 | tf_op jit(solution)/shard_map/all_to_all | solution.py:33
  482.4 5.2 all-to-all-start.2
  487.7 189.9 %all_gather.6 = bf16[2048,16]{0,1:T(8,128)(2,1)S(1)} all-gather(bf16[256,16]{0,1:T(8,128)(2,1)S(1)} %multiply_convert_fusion), channel_id=1, replica_groups=mesh['owner'=4,'rows'=8] {'rows'}, dimensions={0}, use_global_device_ids=true | all-gather | bytes 73728 | tf_op jit(solution)/shard_map/all_gather | solution.py:46
  677.6 8.9 %all_gather.7 = bf16[2048,64]{0,1:T(8,128)(2,1)S(1)} all-gather(bf16[2048,16]{0,1:T(8,128)(2,1)S(1)} %all_gather.6), channel_id=1, replica_groups=mesh['owner'=4,'rows'=8] {'owner'}, dimensions={1}, use_global_device_ids=true | all-gather | bytes 327680 | tf_op jit(solution)/shard_map/all_gather | solution.py:47
  686.5 0.6 constant_dynamic-slice_fusion
  687.1 0.6 constant_dynamic-slice_fusion.1
  687.7 0.6 constant_dynamic-slice_fusion.2
  688.3 7.9 %copy.15 = bf16[16,8,256,128]{3,2,1,0:T(8,128)(2,1)} copy(bf16[16,8,256,128]{3,2,0,1:T(8,128)(2,1)} %bitcast.8) | data formatting | bytes 16777216 | tf_op jit(solution)/shard_map/reshape | solution.py:27
  696.2 12.3 %copy.18 = bf16[16,8,256,128]{3,2,1,0:T(8,128)(2,1)} copy(bf16[16,8,256,128]{2,0,3,1:T(8,128)(2,1)} %bitcast.11) | data formatting | bytes 16777216 | tf_op jit(solution)/shard_map/all_to_all | solution.py:33
  708.5 11.4 %copy.21 = bf16[16,128,8,256]{3,2,1,0:T(8,128)(2,1)} copy(bf16[16,128,8,256]{3,0,1,2:T(8,128)(2,1)} %bitcast.14) | data formatting | bytes 16777216 | tf_op jit(solution)/shard_map/all_to_all | solution.py:35
  719.8 13.4 %all_to_all.37 = bf16[16,128,2048]{2,1,0:T(8,128)(2,1)} reshape(bf16[16,128,8,256]{3,2,1,0:T(8,128)(2,1)} %copy.21) | data formatting | bytes 16777216 | tf_op jit(solution)/shard_map/all_to_all | solution.py:35
  733.3 0.7 copy.36
  (15 shorter events, 0.3 us)
Async XLA Ops:
  7.2 79.6 %all-reduce.3.cloned.1.call-start = ((), (), s32[]{:S(2)}) async-start(), calls=%async_computation.3 | async-start | bytes 393216 | tf_op jit(solution)/shard_map/psum | solution.py:10
  104.8 188.8 %all-to-all-start = ((bf16[8,16,256,128]{3,2,1,0:T(8,128)(2,1)}), bf16[8,16,256,128]{3,2,1,0:T(8,128)(2,1)}, u32[]{:S(2)}, u32[]{:S(2)}) async-start(bf16[8,16,256,128]{3,2,1,0:T(8,128)(2,1)} %fusion.1), calls=%async_computation | async-start | bytes 16777216 | tf_op jit(solution)/shard_map/all_to_all | solution.py:28
  109.8 17.6 %copy-start.1 = (f32[16,1024]{1,0:T(8,128)S(1)}, f32[16,1024]{1,0:T(8,128)}, u32[]{:S(2)}) copy-start(f32[16,1024]{1,0:T(8,128)} %get-tuple-element.8) | copy-start | bytes 196612
  137.3 161.3 %copy-start = (f32[16,1024]{1,0:T(8,128)S(1)}, f32[16,1024]{1,0:T(8,128)}, u32[]{:S(2)}) copy-start(f32[16,1024]{1,0:T(8,128)} %get-tuple-element.9) | copy-start | bytes 196612
  293.6 188.8 %all-to-all-start.1 = ((bf16[16,256,1024]{1,0,2:T(8,128)(2,1)}), bf16[16,256,1024]{1,0,2:T(8,128)(2,1)}, u32[]{:S(2)}, u32[]{:S(2)}) async-start(bf16[16,256,1024]{1,0,2:T(8,128)(2,1)} %divide_convert_fusion), calls=%async_computation.1 | async-start | bytes 16777216 | tf_op jit(solution)/shard_map/all_to_all | solution.py:33
  315.5 172.2 %copy-start.2 = (f32[256,16]{0,1:T(8,128)S(1)}, f32[256,16]{0,1:T(8,128)}, u32[]{:S(2)}) copy-start(f32[256,16]{0,1:T(8,128)} %param.8) | copy-start | bytes 49156
  315.5 172.2 %copy-start.3 = (f32[256]{0:T(256)S(1)}, f32[256]{0:T(256)}, u32[]{:S(2)}) copy-start(f32[256]{0:T(256)} %param.9) | copy-start | bytes 3076
  482.4 226.0 %all-to-all-start.2 = ((bf16[16,1024,256]{2,0,1:T(8,128)(2,1)}), bf16[16,1024,256]{2,0,1:T(8,128)(2,1)}, u32[]{:S(2)}, u32[]{:S(2)}) async-start(bf16[16,1024,256]{2,0,1:T(8,128)(2,1)} %fusion), calls=%async_computation.2 | async-start | bytes 16777216 | tf_op jit(solution)/shard_map/all_to_all | solution.py:35
Sparse Core Ops, SparseCore 0:
  28.6 58.1 all-reduce.2
